TPU v7x, 256 devices: a whole 4x4x8 slice. The times are simulated.
256 devices in a mesh: gx: 32 (over x, y, core), gy: 8 (over z).
Axes of the slice: x: 4, y: 4, z: 8, core: 2. Of those that a mesh axis runs over, the one named last changes fastest.
Arguments:
- fields: float32 [8, 2048, 2048], P(None, 'gx', 'gy'), may hold values from -6 to 6
- wave_order: int32 [1024], replicated, may hold values from 0 to 1023, as said below
- kept_mask: int32 [1024, 2048], P('gx', 'gy'), may hold values from 0 to 1, as said below
Outputs:
- spectral: float32 [2, 8, 1024, 2048], P(None, None, 'gx', 'gy')
Inputs may be any that keep to these rules, and one draw needn't show every extreme that they name: `wave_order`: each x-wavenumber 0 to 1023 once. `kept_mask`: in each row the kept y-wavenumbers q are those with min(q, 2048 - q) up to a bound that does not grow with the row's x-wavenumber.
All inputs are finite; a program needn't handle non-finite values.
Results may differ from a plain program's by a relative error of at most 0.00007.
Values sent between devices are 32-bit elements; how exact they have to be, the bound alone decides.
A program may use at most 192 MiB of HBM per device.

v0:
```python
import math

import jax
import jax.numpy as jnp
from jax import lax
from jax.sharding import PartitionSpec as P

NX = 2048
NY = 2048


def wave_angles(wave_ids, points, period):
    phases = wave_ids[:, None] * points[None, :] % period
    angles = phases.astype(jnp.float32) * (2.0 * math.pi / period)
    return (jnp.cos(angles), jnp.sin(angles))


def x_terms(cos_table, sin_table, values):
    stack_count, x_count, y_count = values.shape
    waves = cos_table.shape[0]
    table = jnp.concatenate([cos_table, -sin_table], axis=0)
    flat = jnp.transpose(values, (1, 0, 2)).reshape(x_count, stack_count * y_count)
    product = jnp.dot(
        table, flat, precision=lax.Precision.HIGHEST, preferred_element_type=jnp.float32
    )
    product = product.reshape(2, waves, stack_count, y_count)
    return jnp.transpose(product, (1, 0, 2, 3))


def y_terms(cos_table, sin_table, spectra):
    rows, parts, stack_count, y_count = spectra.shape
    waves = cos_table.shape[0]
    table = jnp.concatenate([cos_table, sin_table], axis=0)
    flat = spectra.reshape(rows * parts * stack_count, y_count)
    product = jnp.dot(
        flat, table.T, precision=lax.Precision.HIGHEST, preferred_element_type=jnp.float32
    )
    product = product.reshape(rows, parts, stack_count, 2, waves)
    real_part = product[:, 0, :, 0] + product[:, 1, :, 1]
    imag_part = product[:, 1, :, 0] - product[:, 0, :, 1]
    return jnp.stack([real_part, imag_part], axis=1)


def shards(fields, wave_order, kept_mask):
    x_local = fields.shape[1]
    y_local = fields.shape[2]
    x_points = lax.axis_index("gx") * x_local + jnp.arange(x_local, dtype=jnp.int32)
    y_points = lax.axis_index("gy") * y_local + jnp.arange(y_local, dtype=jnp.int32)
    cos_table, sin_table = wave_angles(wave_order, x_points, NX)
    spectra = lax.psum_scatter(
        x_terms(cos_table, sin_table, fields), "gx", scatter_dimension=0, tiled=True
    )
    y_waves = jnp.arange(lax.axis_size("gy") * y_local, dtype=jnp.int32)
    cos_table, sin_table = wave_angles(y_waves, y_points, NY)
    scattered = lax.psum_scatter(
        jnp.transpose(y_terms(cos_table, sin_table, spectra), (3, 1, 2, 0)),
        "gy",
        scatter_dimension=0,
        tiled=True,
    )
    result = jnp.transpose(scattered, (3, 1, 2, 0))
    weight = kept_mask.astype(jnp.float32) * (1.0 / math.sqrt(NX * NY))
    arranged = jnp.transpose(result, (1, 2, 0, 3)) * weight[None, None]
    return arranged


def solution(mesh):
    return jax.shard_map(
        shards,
        mesh=mesh,
        in_specs=(P(None, "gx", "gy"), P(), P("gx", "gy")),
        out_specs=P(None, None, "gx", "gy"),
        check_vma=False,
    )
```

profile of v0, /device:TPU:1, one launch (start us, length us, event | category | flops | bytes accessed | tf_op | source)
XLA Modules:
  0.0 250.3 jit_solution(6958633559297715028)
XLA Ops:
  6.5 0.0 reduce-scatter.3.cloned.1.call-start
  6.5 1.3 copy.19
  7.9 2.8 %fusion.18 = (f32[1024,64]{1,0:T(8,128)S(1)}, f32[1024,64]{1,0:T(8,128)S(1)}) fusion(s32[64]{0:T(128)S(1)} %iota_add_fusion.1, s32[1024]{0:T(1024)} %param.4), kind=kLoop, calls=%fused_computation.35 | loop fusion | flops 983040 | bytes 528640 | tf_op jit(solution)/shard_map/cos | solution.py:15
  10.7 0.1 pad_maximum_fusion.1
  10.8 13.4 %fusion.16 = f32[2,1024,8,256]{3,1,2,0:T(8,128)S(1)} fusion(f32[2,1024,64,1]{2,1,3,0:T(8,128)S(1)} %bitcast.51, f32[8,256,64,1]{1,0,2,3:T(8,128)S(1)} %bitcast.53), kind=kOutput, calls=%fused_computation.32 | convolution fusion | flops 3221225472 | bytes 17825792 | tf_op jit(solution)/shard_map/dot_general | solution.py:23
  24.2 22.9 %copy.24 = f32[2,1024,8,256]{3,2,0,1:T(8,128)} copy(f32[2,1024,8,256]{3,1,2,0:T(8,128)S(1)} %fusion.16) | data formatting | bytes 33554432 | tf_op jit(solution)/shard_map/dot_general | solution.py:23
  47.1 0.0 reduce-scatter.3.cloned.1.call-update
  47.1 0.3 reduce-scatter.5.cloned.1.call-start
  47.4 8.2 %fusion.10 = (f32[2048,256]{1,0:T(8,128)S(1)}, f32[2048,256]{1,0:T(8,128)S(1)}) fusion(s32[256]{0:T(256)S(1)} %iota_add_fusion), kind=kLoop, calls=%fused_computation.20 | loop fusion | flops 7340032 | bytes 4195328 | tf_op jit(solution)/shard_map/cos | solution.py:15
  55.5 2.2 pad_maximum_fusion
  57.8 114.9 %reduce-scatter.3.cloned.1.call-done = f32[32,2,8,256]{3,2,1,0:T(8,128)} async-done(((f32[1024,2,8,256]{3,2,1,0:T(8,128)}), f32[32,2,8,256]{3,2,1,0:T(8,128)}) %reduce-scatter.3.cloned.1.call-update) | async-done | bytes 524304 | tf_op jit(solution)/shard_map/reduce_scatter | solution.py:50
  172.6 9.3 %fusion.14 = f32[32,2,8,2,2048]{4,2,3,1,0:T(8,128)S(1)} fusion(f32[2,2048,256,1,1]{2,1,0,4,3:T(8,128)} %bitcast.52, f32[32,2,8,256]{3,2,1,0:T(8,128)} %reduce-scatter.3.cloned.1.call-done), kind=kOutput, calls=%fused_computation.29 | convolution fusion | flops 6442450944 | bytes 13107200 | tf_op jit(solution)/shard_map/dot_general | solution.py:35
  181.9 0.3 fusion.3
  182.3 0.3 fusion.5
  182.6 2.4 maximum_bitcast_fusion
  185.1 0.0 copy-start
  185.1 0.0 reduce-scatter.5.cloned.1.call-update
  185.1 0.7 copy-done
  185.8 55.6 %reduce-scatter.5.cloned.1.call-done = f32[256,2,8,32]{0,2,3,1:T(8,128)} async-done(((f32[2048,2,8,32]{0,2,3,1:T(8,128)}), f32[256,2,8,32]{0,2,3,1:T(8,128)}) %reduce-scatter.5.cloned.1.call-update) | async-done | bytes 524304 | tf_op jit(solution)/shard_map/reduce_scatter | solution.py:55
  241.4 1.1 bitcast_multiply_fusion
  242.5 1.0 copy.10
  (3 shorter events, 0.0 us)
Async XLA Ops:
  6.5 166.1 %reduce-scatter.3.cloned.1.call-start = ((), (), s32[]{:S(2)}) async-start(), calls=%async_computation.2 | async-start | bytes 17301504 | tf_op jit(solution)/shard_map/reduce_scatter | solution.py:50
  47.1 194.3 %reduce-scatter.5.cloned.1.call-start = ((), (), s32[]{:S(2)}) async-start(), calls=%async_computation.3 | async-start | bytes 4718592 | tf_op jit(solution)/shard_map/reduce_scatter | solution.py:55
  185.1 0.8 copy-start
Sparse Core Ops, SparseCore 0:
  47.2 125.3 reduce-scatter.2
  185.2 56.1 reduce-scatter.4
where the time goes:
time: 251 us; the launch traced here: 250 us
  waiting for transfers between devices  170 us (68%)
  local copies, waits for them, and re-layouts  25.9 us (10%)
  matrix products  22.7 us (9%)
  other arithmetic  17.5 us (7%)
  between operations  13.5 us (5%)
    reduce_scatter x1, waiting for transfers between devices, shards(): lax.psum_scatter(x_terms(cos_table, sin_table, fields), 'gx', scatter_dim...  115 us
    reduce_scatter x1, waiting for transfers between devices, shards(): lax.psum_scatter(jnp.transpose(y_terms(cos_table, sin_table, spectra), (3...  55.6 us
    dot_general x1, local copies, waits for them, and re-layouts, x_terms(): jnp.dot(table, flat, precision=lax.Precision.HIGHEST, preferred_element_t...  22.9 us
    dot_general x1, matrix products, x_terms(): jnp.dot(table, flat, precision=lax.Precision.HIGHEST, preferred_element_t...  13.4 us
    cos x2, other arithmetic, wave_angles(): return (jnp.cos(angles), jnp.sin(angles))  11 us
    dot_general x1, matrix products, y_terms(): jnp.dot(flat, table.T, precision=lax.Precision.HIGHEST, preferred_element...  9.31 us
  transfers between devices with their start and end apart: 2, of which 2 were waited for; matrix products, arithmetic and copies ran while one was open for 4% of the time, Pallas kernels for 0%

commit v1 on v0

v1 whole, which is shorter than its diff:
```python
import functools
import math

import jax
import jax.numpy as jnp
import numpy as np
from jax import lax
from jax.experimental import pallas as pl
from jax.experimental.pallas import tpu as pltpu
from jax.sharding import PartitionSpec as P

MESH = pl.DeviceIdType.MESH
F32 = jnp.float32
BF16 = jnp.bfloat16
N = 2048
GX = 32
GY = 8


def split(value):
    high = value.astype(BF16)
    return high, (value - high.astype(F32)).astype(BF16)


def cos_sin(phase):
    quarter = (phase + 256) >> 9
    rest = (phase - (quarter << 9)).astype(F32) * (2.0 * math.pi / N)
    square = rest * rest
    sine = rest * (
        1.0 + square * (-1.0 / 6 + square * (1.0 / 120 + square * (-1.0 / 5040 + square * (1.0 / 362880))))
    )
    cosine = 1.0 + square * (
        -0.5 + square * (1.0 / 24 + square * (-1.0 / 720 + square * (1.0 / 40320 - square * (1.0 / 3628800))))
    )
    odd = (quarter & 1) == 1
    turn = quarter & 3
    real = jnp.where(odd, sine, cosine)
    imag = jnp.where(odd, cosine, sine)
    real = jnp.where((turn == 1) | (turn == 2), -real, real)
    imag = jnp.where(turn >= 2, -imag, imag)
    return real, imag


def eight_points(values):
    def two(a, b):
        return (a[0] + b[0], a[1] + b[1]), (a[0] - b[0], a[1] - b[1])

    def four(v):
        s0, d0 = two(v[0], v[2])
        s1, d1 = two(v[1], v[3])
        y0, y2 = two(s0, s1)
        y1 = (d0[0] + d1[1], d0[1] - d1[0])
        y3 = (d0[0] - d1[1], d0[1] + d1[0])
        return [y0, y1, y2, y3]

    even = four(values[0::2])
    odd = four(values[1::2])
    root = math.sqrt(0.5)
    r, i = odd[1]
    odd[1] = ((r + i) * root, (i - r) * root)
    r, i = odd[2]
    odd[2] = (i, -r)
    r, i = odd[3]
    odd[3] = ((i - r) * root, (-r - i) * root)
    pairs = [two(a, b) for a, b in zip(even, odd)]
    return [p[0] for p in pairs] + [p[1] for p in pairs]


def kernel(
    fields_ref, wave_ref, mask_ref, w_ref, twiddle_ref, out_ref,
    send1, recv1, base_re, base_im, tabs, ft, ftp, send2, recv2, ybuf, send3, recv3,
    s1, r1, s2, r2, s3, r3,
):
    g = lax.axis_index("gx")
    z = lax.axis_index("gy")
    level = g // 4
    lane = lax.broadcasted_iota(jnp.int32, (16, 128), 1)
    low = lane < 64

    def pack(s, carry):
        for j in range(2):
            part = [fields_ref[s, pl.ds(16 * h, 16), pl.ds(128 * j, 128)] for h in range(4)]
            turned = [pltpu.roll(p, 64, 1) for p in part]
            for half in range(2):
                send1[4 * s + 2 * j, :, pl.ds(128 * half, 128)] = jnp.where(low, part[2 * half], turned[2 * half + 1])
                send1[4 * s + 2 * j + 1, :, pl.ds(128 * half, 128)] = jnp.where(low, turned[2 * half], part[2 * half + 1])
        return carry

    lax.fori_loop(0, 8, pack, 0)

    def copy1(src, dst_slot, peer):
        return pltpu.make_async_remote_copy(
            src_ref=send1.at[src], dst_ref=recv1.at[dst_slot], send_sem=s1.at[src], recv_sem=r1.at[dst_slot],
            device_id=(peer, z), device_id_type=MESH,
        )

    def start1(d, carry):
        peer = lax.rem(g + d, GX)
        copy1(peer, g, peer).start()
        return carry

    lax.fori_loop(1, GX, start1, 0)
    recv1[g] = send1[g]

    waves = wave_ref[0:1, :]
    rows = lax.broadcasted_iota(jnp.int32, (56, 1024), 0)
    steps = jnp.where(rows < 32, rows * 64, jnp.where(rows < 48, rows - 32, (rows - 48) * 16))
    real, imag = cos_sin((steps * waves) & (N - 1))
    base_re[...] = real
    base_im[...] = imag

    def table(step, carry):
        group, c = step // 8, lax.rem(step, 8)
        cols = pl.ds(pl.multiple_of(128 * c, 128), 128)
        tile = pl.ds(pl.multiple_of(8 * group, 8), 8)
        tile_re, tile_im = base_re[tile, cols], base_im[tile, cols]
        br, bi = base_re[32:48, cols], base_im[32:48, cols]
        for i in range(8):
            ar, ai = tile_re[i : i + 1], tile_im[i : i + 1]
            re_hi, re_lo = split(ar * br - ai * bi)
            im_hi, im_lo = split(-(ar * bi + ai * br))
            at = pl.multiple_of(group * 128 + i * 16, 16)
            tabs[c, pl.ds(at, 16), 0:128] = re_hi
            tabs[c, pl.ds(at, 16), 128:256] = im_hi
            tabs[c, pl.ds(at + 512, 16), 0:128] = re_lo
            tabs[c, pl.ds(at + 512, 16), 128:256] = im_lo
        return carry

    lax.fori_loop(0, 32, table, 0)

    def wait1(d, carry):
        peer = lax.rem(g + d, GX)
        copy1(peer, peer, peer).wait_recv()
        return carry

    lax.fori_loop(1, GX, wait1, 0)

    for i in range(4):
        ft[:, :, pl.ds(128 * i, 128)] = recv1[8 * i : 8 * i + 8].reshape(128, 256).T.reshape(32, 8, 128)
    for h in range(4):
        for v in range(8):
            ftp[pl.ds(64 * h + 8 * v, 8), :] = ft[8 * h : 8 * h + 8, v, :]
    hi, lo = split(ftp[...])
    wide = jnp.concatenate([hi, hi], axis=1)
    lane32 = lax.broadcasted_iota(jnp.int32, (32, 128), 1)
    below = lane32 < 64
    even = (lane32 & 32) == 0

    def copy2(row_owner, slot, zz):
        return pltpu.make_async_remote_copy(
            src_ref=send2.at[row_owner], dst_ref=recv2.at[slot], send_sem=s2.at[row_owner], recv_sem=r2.at[slot],
            device_id=(row_owner, zz), device_id_type=MESH,
        )

    my_slot = 4 * z + lax.rem(g, 4)

    def chunk(step, carry):
        c = lax.rem(step + level, 8)
        sums = jnp.dot(wide, tabs[c], preferred_element_type=F32)
        sums = sums + jnp.dot(lo, tabs[c, 0:512, :], preferred_element_type=F32)
        cols = pl.ds(pl.multiple_of(128 * c, 128), 128)
        xr, xi = sums[0:64, 0:128], sums[0:64, 128:256]
        for h in range(1, 4):
            gr, gi = sums[64 * h : 64 * h + 64, 0:128], sums[64 * h : 64 * h + 64, 128:256]
            cr, ci = base_re[48 + h : 49 + h, cols], base_im[48 + h : 49 + h, cols]
            xr = xr + gr * cr + gi * ci
            xi = xi + gi * cr - gr * ci
        xr = xr.reshape(4, 2, 8, 128)
        xi = xi.reshape(4, 2, 8, 128)
        v = [x[:, j].reshape(32, 128) for j in range(2) for x in (xr, xi)]
        out = [None] * 4
        for d1 in range(2):
            pair = []
            for m0 in range(2):
                a, b = v[m0], v[m0 + 2]
                pair.append(jnp.where(below, a, pltpu.roll(b, 64, 1)) if d1 == 0 else jnp.where(below, pltpu.roll(a, 64, 1), b))
            a, b = pair
            out[2 * d1] = jnp.where(even, a, pltpu.roll(b, 32, 1))
            out[2 * d1 + 1] = jnp.where(even, pltpu.roll(a, 96, 1), b)
        for d in range(4):
            send2[4 * c + d] = out[d].reshape(4, 8, 128)
        for d in range(4):
            owner = 4 * c + d
            mine = (owner == g) & (level == z)

            @pl.when(jnp.logical_not(mine))
            def _():
                copy2(owner, my_slot, level).start()

            @pl.when(mine)
            def _():
                recv2[my_slot] = send2[owner]

        return carry

    lax.fori_loop(0, 8, chunk, 0)

    def wait2(slot, carry):
        source = 4 * z + lax.rem(slot, 4)
        mine = (source == g) & (slot // 4 == z)

        @pl.when(jnp.logical_not(mine))
        def _():
            copy2(0, slot, z).wait_recv()

        return carry

    lax.fori_loop(0, 32, wait2, 0)

    for t in range(4):
        lines = recv2[:, t].reshape(256, 128).T
        hi, lo = split(lines)
        both = jnp.concatenate([hi, hi, lo], axis=1)
        ybuf[pl.ds(128 * t, 128), :] = jnp.dot(both, w_ref[...], preferred_element_type=F32)

    def finish(tile, carry):
        at = pl.multiple_of(8 * tile, 8)
        values = []
        for v in range(8):
            rr = ybuf[pl.ds(64 * v + at, 8), :]
            ii = ybuf[pl.ds(64 * v + 32 + at, 8), :]
            re = rr[:, :256] - ii[:, 256:]
            im = rr[:, 256:] + ii[:, :256]
            c, s = twiddle_ref[v : v + 1, :], twiddle_ref[8 + v : 9 + v, :]
            values.append((re * c + im * s, im * c - re * s))
        for q, (re, im) in enumerate(eight_points(values)):
            send3[q, 0, pl.ds(at, 8), :] = re
            send3[q, 1, pl.ds(at, 8), :] = im
        return carry

    lax.fori_loop(0, 4, finish, 0)

    def copy3(src, slot, peer):
        return pltpu.make_async_remote_copy(
            src_ref=send3.at[src], dst_ref=recv3.at[slot], send_sem=s3.at[src], recv_sem=r3.at[slot],
            device_id=(g, peer), device_id_type=MESH,
        )

    for d in range(1, GY):
        peer = lax.rem(z + d, GY)
        copy3(peer, z, peer).start()
    weight = mask_ref[...].astype(F32)
    for p in range(2):
        out_ref[p, z] = send3[z, p] * weight
    for d in range(1, GY):
        peer = lax.rem(z + d, GY)
        copy3(peer, peer, peer).wait_recv()
        for p in range(2):
            out_ref[p, peer] = recv3[peer, p] * weight

    def drain1(d, carry):
        peer = lax.rem(g + d, GX)
        copy1(peer, peer, peer).wait_send()
        return carry

    lax.fori_loop(1, GX, drain1, 0)

    def drain2(owner, carry):
        mine = (owner == g) & (level == z)

        @pl.when(jnp.logical_not(mine))
        def _():
            copy2(owner, my_slot, level).wait_send()

        return carry

    lax.fori_loop(0, 32, drain2, 0)
    for d in range(1, GY):
        peer = lax.rem(z + d, GY)
        copy3(peer, peer, peer).wait_send()


def y_tables():
    turns = np.outer(np.arange(256), np.arange(256)) % 256 * (2.0 * np.pi / 256)
    table = np.concatenate([np.cos(turns), -np.sin(turns)], axis=1).astype(np.float32)
    high = table.astype(jnp.bfloat16)
    low = (table - high.astype(np.float32)).astype(jnp.bfloat16)
    angles = np.outer(np.arange(8), np.arange(256)) * (2.0 * np.pi / N)
    twiddle = np.concatenate([np.cos(angles), np.sin(angles)]) / N
    return np.concatenate([high, low, high], axis=0), twiddle.astype(np.float32)


def shards(fields, wave_order, kept_mask):
    w, twiddle = y_tables()
    vmem = pl.BlockSpec(memory_space=pltpu.VMEM)
    dma = pltpu.SemaphoreType.DMA
    return pl.pallas_call(
        kernel,
        out_shape=jax.ShapeDtypeStruct((2, 8, 32, 256), F32),
        in_specs=[vmem] * 5,
        out_specs=vmem,
        scratch_shapes=[
            pltpu.VMEM((32, 16, 256), F32),
            pltpu.VMEM((32, 16, 256), F32),
            pltpu.VMEM((56, 1024), F32),
            pltpu.VMEM((56, 1024), F32),
            pltpu.VMEM((8, 1024, 256), BF16),
            pltpu.VMEM((32, 8, 512), F32),
            pltpu.VMEM((256, 512), F32),
            pltpu.VMEM((32, 4, 8, 128), F32),
            pltpu.VMEM((32, 4, 8, 128), F32),
            pltpu.VMEM((512, 512), F32),
            pltpu.VMEM((8, 2, 32, 256), F32),
            pltpu.VMEM((8, 2, 32, 256), F32),
            dma((32,)), dma((32,)), dma((32,)), dma((32,)), dma((8,)), dma((8,)),
        ],
        compiler_params=pltpu.CompilerParams(has_side_effects=True, vmem_limit_bytes=48 * 1024 * 1024),
        name="bifourier",
    )(fields, wave_order.reshape(1, 1024), kept_mask, jnp.asarray(w), jnp.asarray(twiddle))


def solution(mesh):
    return jax.shard_map(
        shards,
        mesh=mesh,
        in_specs=(P(None, "gx", "gy"), P(), P("gx", "gy")),
        out_specs=P(None, None, "gx", "gy"),
        check_vma=False,
    )
```

time: 251 us -> 100 us (0.40)
  waiting for transfers between devices: 170 us -> 0 us
  Pallas kernels: 0 us -> 93.9 us
  matrix products: 22.7 us -> 0 us
  local copies, waits for them, and re-layouts: 25.9 us -> 5.13 us
  other arithmetic: 17.5 us -> 0 us
  between operations: 13.5 us -> 0.01 us
    reduce_scatter x2 -> x0, waiting for transfers between devices: 170 us -> none  [the longest x1 115 us: shards(): lax.psum_scatter(x_terms(cos_table, sin_table, fields), 'gx', scatter_dim...]
    pallas_call x0 -> x1, Pallas kernels: none -> 93.9 us  [shards(): pl.pallas_call(kernel, out_shape=jax.ShapeDtypeStruct((2, 8, 32, 256), F3...]
    dot_general x1 -> x0, local copies, waits for them, and re-layouts: 22.9 us -> none  [x_terms(): jnp.dot(table, flat, precision=lax.Precision.HIGHEST, preferred_element_t...]
    dot_general x2 -> x0, matrix products: 22.7 us -> none  [the longest x1 13.4 us: x_terms(): jnp.dot(table, flat, precision=lax.Precision.HIGHEST, preferred_element_t...]
    cos x2 -> x0, other arithmetic: 11 us -> none  [wave_angles(): return (jnp.cos(angles), jnp.sin(angles))]
    unnamed x3 -> x11, local copies, waits for them, and re-layouts: 2.08 us -> 5.13 us
  transfers between devices with their start and end apart: 2 -> 0, of which waited for: 2 -> 0; matrix products, arithmetic and copies ran while one was open for 4% -> 0% of each run, Pallas kernels for 0% -> 0%
where the time goes in v1:
time: 100 us; the launch traced here: 99.1 us
  Pallas kernels  93.9 us (94%)
  local copies, waits for them, and re-layouts  5.13 us (5%)
    pallas_call x1, Pallas kernels, shards(): pl.pallas_call(kernel, out_shape=jax.ShapeDtypeStruct((2, 8, 32, 256), F3...  93.9 us
    unnamed x11, local copies, waits for them, and re-layouts  5.13 us

profile of v1, /device:TPU:1, one launch (start us, length us, event | category | flops | bytes accessed | tf_op | source)
XLA Modules:
  0.0 99.1 jit_solution(14590339203111415530)
XLA Ops:
  0.0 0.0 copy-start
  0.0 1.1 %copy-done = bf16[768,512]{1,0:T(8,128)(2,1)S(1)} copy-done((bf16[768,512]{1,0:T(8,128)(2,1)S(1)}, bf16[768,512]{1,0:T(8,128)(2,1)}, u32[]{:S(2)}) %copy-start) | copy-done | bytes 786456
  1.1 0.0 copy-start.1
  1.1 1.0 %copy-done.1 = f32[8,64,256]{2,1,0:T(8,128)S(1)} copy-done((f32[8,64,256]{2,1,0:T(8,128)S(1)}, f32[8,64,256]{2,1,0:T(8,128)}, u32[]{:S(2)}) %copy-start.1) | copy-done | bytes 524312
  2.2 0.0 copy-start.2
  2.2 0.8 copy-done.2
  2.9 0.0 copy-start.3
  2.9 0.7 copy-done.3
  3.7 0.0 copy-start.4
  3.7 0.7 copy-done.4
  4.3 93.9 %bifourier.1 = f32[2,8,32,256]{3,2,1,0:T(8,128)S(1)} custom-call(f32[8,64,256]{2,1,0:T(8,128)S(1)} %copy-done.1, s32[1,1024]{1,0:T(1,128)S(1)} %bitcast.1, s32[32,256]{1,0:T(8,128)S(1)} %copy-done.2, bf16[768,512]{1,0:T(8,128)(2,1)S(1)} %copy-done, f32[16,256]{1,0:T(8,128)S(1)} %copy-done.3), custom_call_target="tpu_custom_call" | custom-call | tf_op jit(solution)/shard_map/bifourier/pallas_call | solution.py:287
  98.3 0.8 copy.7
Async XLA Ops:
  0.0 1.1 %copy-start = (bf16[768,512]{1,0:T(8,128)(2,1)S(1)}, bf16[768,512]{1,0:T(8,128)(2,1)}, u32[]{:S(2)}) copy-start(bf16[768,512]{1,0:T(8,128)(2,1)} %constant.4.clone.w_ref) | copy-start | bytes 2359300
  1.1 1.0 %copy-start.1 = (f32[8,64,256]{2,1,0:T(8,128)S(1)}, f32[8,64,256]{2,1,0:T(8,128)}, u32[]{:S(2)}) copy-start(f32[8,64,256]{2,1,0:T(8,128)} %fields_ref.1) | copy-start | bytes 1572868
  2.2 0.8 copy-start.2
  2.9 0.7 copy-start.3
  3.7 0.7 copy-start.4

commit v2 on v1

--- a/solution.py
+++ b/solution.py
@@ -67,13 +67,35 @@
 
 
 def kernel(
-    fields_ref, wave_ref, mask_ref, w_ref, twiddle_ref, out_ref,
+    fields_hbm, wave_hbm, mask_hbm, w_hbm, twiddle_hbm, out_ref,
+    fields_ref, wave_ref, mask_ref, w_ref, twiddle_ref, load,
     send1, recv1, base_re, base_im, tabs, ft, ftp, send2, recv2, ybuf, send3, recv3,
     s1, r1, s2, r2, s3, r3,
 ):
     g = lax.axis_index("gx")
     z = lax.axis_index("gy")
     level = g // 4
+    my_level = lax.rem(z + GY - level, GY)
+
+    loads = [
+        pltpu.make_async_copy(source, target, load.at[i])
+        for i, (source, target) in enumerate(
+            [(fields_hbm, fields_ref), (wave_hbm, wave_ref), (mask_hbm, mask_ref), (w_hbm, w_ref), (twiddle_hbm, twiddle_ref)]
+        )
+    ]
+    for copy in loads:
+        copy.start()
+
+    barrier = pltpu.get_barrier_semaphore()
+
+    def greet(d, carry):
+        pl.semaphore_signal(barrier, inc=1, device_id=(lax.rem(g + d, GX), z), device_id_type=MESH)
+        return carry
+
+    lax.fori_loop(1, GX, greet, 0)
+    for d in range(1, GY):
+        pl.semaphore_signal(barrier, inc=1, device_id=(g, lax.rem(z + d, GY)), device_id_type=MESH)
+    loads[0].wait()
     lane = lax.broadcasted_iota(jnp.int32, (16, 128), 1)
     low = lane < 64
 
@@ -99,9 +121,11 @@
         copy1(peer, g, peer).start()
         return carry
 
+    pl.semaphore_wait(barrier, GX - 1 + GY - 1)
     lax.fori_loop(1, GX, start1, 0)
     recv1[g] = send1[g]
 
+    loads[1].wait()
     waves = wave_ref[0:1, :]
     rows = lax.broadcasted_iota(jnp.int32, (56, 1024), 0)
     steps = jnp.where(rows < 32, rows * 64, jnp.where(rows < 48, rows - 32, (rows - 48) * 16))
@@ -181,11 +205,12 @@
             send2[4 * c + d] = out[d].reshape(4, 8, 128)
         for d in range(4):
             owner = 4 * c + d
-            mine = (owner == g) & (level == z)
+            place = lax.rem(level + c, GY)
+            mine = (owner == g) & (place == z)
 
             @pl.when(jnp.logical_not(mine))
             def _():
-                copy2(owner, my_slot, level).start()
+                copy2(owner, my_slot, place).start()
 
             @pl.when(mine)
             def _():
@@ -196,7 +221,7 @@
     lax.fori_loop(0, 8, chunk, 0)
 
     def wait2(slot, carry):
-        source = 4 * z + lax.rem(slot, 4)
+        source = 4 * my_level + lax.rem(slot, 4)
         mine = (source == g) & (slot // 4 == z)
 
         @pl.when(jnp.logical_not(mine))
@@ -207,6 +232,9 @@
 
     lax.fori_loop(0, 32, wait2, 0)
 
+    loads[3].wait()
+    loads[4].wait()
+    loads[2].wait()
     for t in range(4):
         lines = recv2[:, t].reshape(256, 128).T
         hi, lo = split(lines)
@@ -241,12 +269,12 @@
         copy3(peer, z, peer).start()
     weight = mask_ref[...].astype(F32)
     for p in range(2):
-        out_ref[p, z] = send3[z, p] * weight
+        out_ref[p, my_level] = send3[z, p] * weight
     for d in range(1, GY):
         peer = lax.rem(z + d, GY)
         copy3(peer, peer, peer).wait_recv()
         for p in range(2):
-            out_ref[p, peer] = recv3[peer, p] * weight
+            out_ref[p, lax.rem(my_level + d, GY)] = recv3[peer, p] * weight
 
     def drain1(d, carry):
         peer = lax.rem(g + d, GX)
@@ -256,11 +284,12 @@
     lax.fori_loop(1, GX, drain1, 0)
 
     def drain2(owner, carry):
-        mine = (owner == g) & (level == z)
+        place = lax.rem(level + owner // 4, GY)
+        mine = (owner == g) & (place == z)
 
         @pl.when(jnp.logical_not(mine))
         def _():
-            copy2(owner, my_slot, level).wait_send()
+            copy2(owner, my_slot, place).wait_send()
 
         return carry
 
@@ -287,9 +316,15 @@
     return pl.pallas_call(
         kernel,
         out_shape=jax.ShapeDtypeStruct((2, 8, 32, 256), F32),
-        in_specs=[vmem] * 5,
+        in_specs=[pl.BlockSpec(memory_space=pltpu.HBM)] * 5,
         out_specs=vmem,
         scratch_shapes=[
+            pltpu.VMEM((8, 64, 256), F32),
+            pltpu.VMEM((1, 1024), jnp.int32),
+            pltpu.VMEM((32, 256), jnp.int32),
+            pltpu.VMEM((768, 512), BF16),
+            pltpu.VMEM((16, 256), F32),
+            dma((5,)),
             pltpu.VMEM((32, 16, 256), F32),
             pltpu.VMEM((32, 16, 256), F32),
             pltpu.VMEM((56, 1024), F32),
@@ -304,7 +339,7 @@
             pltpu.VMEM((8, 2, 32, 256), F32),
             dma((32,)), dma((32,)), dma((32,)), dma((32,)), dma((8,)), dma((8,)),
         ],
-        compiler_params=pltpu.CompilerParams(has_side_effects=True, vmem_limit_bytes=48 * 1024 * 1024),
+        compiler_params=pltpu.CompilerParams(has_side_effects=True, collective_id=0, vmem_limit_bytes=48 * 1024 * 1024),
         name="bifourier",
     )(fields, wave_order.reshape(1, 1024), kept_mask, jnp.asarray(w), jnp.asarray(twiddle))
 

time: 100 us -> 59.4 us (0.59)
  Pallas kernels: 93.9 us -> 53.4 us
    pallas_call x1, Pallas kernels: 93.9 us -> 53.4 us  [shards(): pl.pallas_call(kernel, out_shape=jax.ShapeDtypeStruct((2, 8, 32, 256), F3...]
where the time goes in v2:
time: 59.4 us; the launch traced here: 58.6 us
  Pallas kernels  53.4 us (90%)
  local copies, waits for them, and re-layouts  5.13 us (9%)
    pallas_call x1, Pallas kernels, shards(): pl.pallas_call(kernel, out_shape=jax.ShapeDtypeStruct((2, 8, 32, 256), F3...  53.4 us
    unnamed x11, local copies, waits for them, and re-layouts  5.13 us

profile of v2, /device:TPU:1, one launch (start us, length us, event | category | flops | bytes accessed | tf_op | source)
XLA Modules:
  0.0 58.6 jit_solution(8331335195234045988)
XLA Ops:
  0.0 0.0 copy-start
  0.0 1.1 %copy-done = bf16[768,512]{1,0:T(8,128)(2,1)S(1)} copy-done((bf16[768,512]{1,0:T(8,128)(2,1)S(1)}, bf16[768,512]{1,0:T(8,128)(2,1)}, u32[]{:S(2)}) %copy-start) | copy-done | bytes 786456
  1.1 0.0 copy-start.1
  1.1 1.0 %copy-done.1 = f32[8,64,256]{2,1,0:T(8,128)S(1)} copy-done((f32[8,64,256]{2,1,0:T(8,128)S(1)}, f32[8,64,256]{2,1,0:T(8,128)}, u32[]{:S(2)}) %copy-start.1) | copy-done | bytes 524312
  2.2 0.0 copy-start.2
  2.2 0.8 %copy-done.2 = s32[32,256]{1,0:T(8,128)S(1)} copy-done((s32[32,256]{1,0:T(8,128)S(1)}, s32[32,256]{1,0:T(8,128)}, u32[]{:S(2)}) %copy-start.2) | copy-done | bytes 32792
  2.9 0.0 copy-start.3
  2.9 0.7 %copy-done.3 = f32[16,256]{1,0:T(8,128)S(1)} copy-done((f32[16,256]{1,0:T(8,128)S(1)}, f32[16,256]{1,0:T(8,128)}, u32[]{:S(2)}) %copy-start.3) | copy-done | bytes 16408
  3.7 0.0 copy-start.4
  3.7 0.7 %copy-done.4 = s32[1024]{0:T(1024)S(1)} copy-done((s32[1024]{0:T(1024)S(1)}, s32[1024]{0:T(1024)}, u32[]{:S(2)}) %copy-start.4) | copy-done | bytes 4120
  4.3 53.4 %bifourier.1 = f32[2,8,32,256]{3,2,1,0:T(8,128)S(1)} custom-call(f32[8,64,256]{2,1,0:T(8,128)S(1)} %copy-done.1, s32[1,1024]{1,0:T(1,128)S(1)} %bitcast.1, s32[32,256]{1,0:T(8,128)S(1)} %copy-done.2, bf16[768,512]{1,0:T(8,128)(2,1)S(1)} %copy-done, f32[16,256]{1,0:T(8,128)S(1)} %copy-done.3), custom_call_target="tpu_custom_call" | custom-call | tf_op jit(solution)/shard_map/bifourier/pallas_call | solution.py:316
  57.8 0.8 %copy.7 = f32[2,8,32,256]{3,2,1,0:T(8,128)} copy(f32[2,8,32,256]{3,2,1,0:T(8,128)S(1)} %bifourier.1) | data formatting | bytes 1048576
Async XLA Ops:
  0.0 1.1 %copy-start = (bf16[768,512]{1,0:T(8,128)(2,1)S(1)}, bf16[768,512]{1,0:T(8,128)(2,1)}, u32[]{:S(2)}) copy-start(bf16[768,512]{1,0:T(8,128)(2,1)} %constant.4.clone.w_hbm) | copy-start | bytes 2359300
  1.1 1.0 %copy-start.1 = (f32[8,64,256]{2,1,0:T(8,128)S(1)}, f32[8,64,256]{2,1,0:T(8,128)}, u32[]{:S(2)}) copy-start(f32[8,64,256]{2,1,0:T(8,128)} %fields_hbm.1) | copy-start | bytes 1572868
  2.2 0.8 %copy-start.2 = (s32[32,256]{1,0:T(8,128)S(1)}, s32[32,256]{1,0:T(8,128)}, u32[]{:S(2)}) copy-start(s32[32,256]{1,0:T(8,128)} %mask_hbm.1) | copy-start | bytes 98308
  2.9 0.7 %copy-start.3 = (f32[16,256]{1,0:T(8,128)S(1)}, f32[16,256]{1,0:T(8,128)}, u32[]{:S(2)}) copy-start(f32[16,256]{1,0:T(8,128)} %constant.5.clone.twiddle_hbm) | copy-start | bytes 49156
  3.7 0.7 %copy-start.4 = (s32[1024]{0:T(1024)S(1)}, s32[1024]{0:T(1024)}, u32[]{:S(2)}) copy-start(s32[1024]{0:T(1024)} %param.6) | copy-start | bytes 12292

commit v3 on v2

--- a/solution.py
+++ b/solution.py
@@ -220,6 +220,13 @@
 
     lax.fori_loop(0, 8, chunk, 0)
 
+    def drain1(d, carry):
+        peer = lax.rem(g + d, GX)
+        copy1(peer, peer, peer).wait_send()
+        return carry
+
+    lax.fori_loop(1, GX, drain1, 0)
+
     def wait2(slot, carry):
         source = 4 * my_level + lax.rem(slot, 4)
         mine = (source == g) & (slot // 4 == z)
@@ -267,6 +274,17 @@
     for d in range(1, GY):
         peer = lax.rem(z + d, GY)
         copy3(peer, z, peer).start()
+    def drain2(owner, carry):
+        place = lax.rem(level + owner // 4, GY)
+        mine = (owner == g) & (place == z)
+
+        @pl.when(jnp.logical_not(mine))
+        def _():
+            copy2(owner, my_slot, place).wait_send()
+
+        return carry
+
+    lax.fori_loop(0, 32, drain2, 0)
     weight = mask_ref[...].astype(F32)
     for p in range(2):
         out_ref[p, my_level] = send3[z, p] * weight
@@ -276,24 +294,6 @@
         for p in range(2):
             out_ref[p, lax.rem(my_level + d, GY)] = recv3[peer, p] * weight
 
-    def drain1(d, carry):
-        peer = lax.rem(g + d, GX)
-        copy1(peer, peer, peer).wait_send()
-        return carry
-
-    lax.fori_loop(1, GX, drain1, 0)
-
-    def drain2(owner, carry):
-        place = lax.rem(level + owner // 4, GY)
-        mine = (owner == g) & (place == z)
-
-        @pl.when(jnp.logical_not(mine))
-        def _():
-            copy2(owner, my_slot, place).wait_send()
-
-        return carry
-
-    lax.fori_loop(0, 32, drain2, 0)
     for d in range(1, GY):
         peer = lax.rem(z + d, GY)
         copy3(peer, peer, peer).wait_send()
@@ -339,7 +339,7 @@
             pltpu.VMEM((8, 2, 32, 256), F32),
             dma((32,)), dma((32,)), dma((32,)), dma((32,)), dma((8,)), dma((8,)),
         ],
-        compiler_params=pltpu.CompilerParams(has_side_effects=True, collective_id=0, vmem_limit_bytes=48 * 1024 * 1024),
+        compiler_params=pltpu.CompilerParams(has_side_effects=True, collective_id=0, vmem_limit_bytes=67043328),
         name="bifourier",
     )(fields, wave_order.reshape(1, 1024), kept_mask, jnp.asarray(w), jnp.asarray(twiddle))
 

time: 59.4 us -> 55.6 us (0.936)
  local copies, waits for them, and re-layouts: 5.13 us -> 1.88 us
    unnamed x11 -> x1, local copies, waits for them, and re-layouts: 5.13 us -> 1.88 us
where the time goes in v3:
time: 55.6 us; the launch traced here: 55 us
  Pallas kernels  53.1 us (96%)
  local copies, waits for them, and re-layouts  1.88 us (3%)
    pallas_call x1, Pallas kernels, shards(): pl.pallas_call(kernel, out_shape=jax.ShapeDtypeStruct((2, 8, 32, 256), F3...  53.1 us
    unnamed x1, local copies, waits for them, and re-layouts  1.88 us

profile of v3, /device:TPU:1, one launch (start us, length us, event | category | flops | bytes accessed | tf_op | source)
XLA Modules:
  0.0 55.0 jit_solution(1873128774091117466)
XLA Ops:
  0.0 53.1 %bifourier.1 = f32[2,8,32,256]{3,2,1,0:T(8,128)} custom-call(f32[8,64,256]{2,1,0:T(8,128)} %fields_hbm.1, s32[1,1024]{1,0:T(1,128)} %bitcast.1, s32[32,256]{1,0:T(8,128)} %mask_hbm.1, bf16[768,512]{1,0:T(8,128)(2,1)} %constant.4.clone.w_hbm, f32[16,256]{1,0:T(8,128)} %constant.5.clone.twiddle_hbm), custom_call_target="tpu_custom_call" | custom-call | tf_op jit(solution)/shard_map/bifourier/pallas_call | solution.py:316
  53.1 1.9 %copy.7 = f32[2,8,32,256]{3,2,1,0:T(8,128)} copy(f32[2,8,32,256]{3,2,1,0:T(8,128)} %bifourier.1) | data formatting | bytes 1048576

commit v4 on v3

v4 whole, which is shorter than its diff:
```python
import functools
import math

import jax
import jax.numpy as jnp
import numpy as np
from jax import lax
from jax.experimental import pallas as pl
from jax.experimental.pallas import tpu as pltpu
from jax.sharding import PartitionSpec as P

MESH = pl.DeviceIdType.MESH
F32 = jnp.float32
BF16 = jnp.bfloat16
N = 2048
GX = 32
GY = 8


def split(value):
    high = value.astype(BF16)
    return high, (value - high.astype(F32)).astype(BF16)


def cos_sin(phase):
    quarter = (phase + 256) >> 9
    rest = (phase - (quarter << 9)).astype(F32) * (2.0 * math.pi / N)
    square = rest * rest
    sine = rest * (
        1.0 + square * (-1.0 / 6 + square * (1.0 / 120 + square * (-1.0 / 5040 + square * (1.0 / 362880))))
    )
    cosine = 1.0 + square * (
        -0.5 + square * (1.0 / 24 + square * (-1.0 / 720 + square * (1.0 / 40320 - square * (1.0 / 3628800))))
    )
    odd = (quarter & 1) == 1
    turn = quarter & 3
    real = jnp.where(odd, sine, cosine)
    imag = jnp.where(odd, cosine, sine)
    real = jnp.where((turn == 1) | (turn == 2), -real, real)
    imag = jnp.where(turn >= 2, -imag, imag)
    return real, imag


def eight_points(values):
    def two(a, b):
        return (a[0] + b[0], a[1] + b[1]), (a[0] - b[0], a[1] - b[1])

    def four(v):
        s0, d0 = two(v[0], v[2])
        s1, d1 = two(v[1], v[3])
        y0, y2 = two(s0, s1)
        y1 = (d0[0] + d1[1], d0[1] - d1[0])
        y3 = (d0[0] - d1[1], d0[1] + d1[0])
        return [y0, y1, y2, y3]

    even = four(values[0::2])
    odd = four(values[1::2])
    root = math.sqrt(0.5)
    r, i = odd[1]
    odd[1] = ((r + i) * root, (i - r) * root)
    r, i = odd[2]
    odd[2] = (i, -r)
    r, i = odd[3]
    odd[3] = ((i - r) * root, (-r - i) * root)
    pairs = [two(a, b) for a, b in zip(even, odd)]
    return [p[0] for p in pairs] + [p[1] for p in pairs]


def swap_blocks(values, lane):
    count = len(values)
    step, width = count // 2, 64
    values = list(values)
    while step:
        first = (lane & width) == 0
        for m in range(count):
            if not m & step:
                a, b = values[m], values[m | step]
                values[m] = jnp.where(first, a, pltpu.roll(b, width, 1))
                values[m | step] = jnp.where(first, pltpu.roll(a, 128 - width, 1), b)
        step, width = step // 2, width // 2
    return values


def kernel(
    fields_hbm, wave_hbm, mask_hbm, w_hbm, twiddle_hbm, out_ref,
    fields_ref, wave_ref, mask_ref, w_ref, twiddle_ref, load,
    send1, recv1, base_re, base_im, tabs, lhs, send2, recv2, ybuf, send3, recv3,
    s1, r1, s2, r2, s3, r3,
):
    g = lax.axis_index("gx")
    z = lax.axis_index("gy")
    level = g // 4
    my_level = lax.rem(z + GY - level, GY)

    loads = [
        pltpu.make_async_copy(source, target, load.at[i])
        for i, (source, target) in enumerate(
            [(fields_hbm, fields_ref), (wave_hbm, wave_ref), (mask_hbm, mask_ref), (w_hbm, w_ref), (twiddle_hbm, twiddle_ref)]
        )
    ]
    for copy in loads:
        copy.start()

    barrier = pltpu.get_barrier_semaphore()

    def greet(d, carry):
        pl.semaphore_signal(barrier, inc=1, device_id=(lax.rem(g + d, GX), z), device_id_type=MESH)
        return carry

    lax.fori_loop(1, GX, greet, 0)
    for d in range(1, GY):
        pl.semaphore_signal(barrier, inc=1, device_id=(g, lax.rem(z + d, GY)), device_id_type=MESH)
    lane = lax.broadcasted_iota(jnp.int32, (8, 128), 1)
    order = (lane & 64) + ((lane & 7) << 3) + ((lane >> 3) & 7)
    loads[0].wait()

    def pack(s, carry):
        for j in range(2):
            for quad in range(2):
                part = [
                    jnp.take_along_axis(fields_ref[s, pl.ds(32 * quad + 8 * h, 8), pl.ds(128 * j, 128)], order, axis=1)
                    for h in range(4)
                ]
                for d, block in enumerate(swap_blocks(part, lane)):
                    send1[d % 2, 4 * s + 2 * j + d // 2, :, pl.ds(128 * quad, 128)] = block
        return carry

    lax.fori_loop(0, 8, pack, 0)

    def copy1(b, src, slot, peer):
        return pltpu.make_async_remote_copy(
            src_ref=send1.at[b, src], dst_ref=recv1.at[b, slot], send_sem=s1.at[b, src], recv_sem=r1.at[b, slot],
            device_id=(peer, z), device_id_type=MESH,
        )

    pl.semaphore_wait(barrier, GX - 1 + GY - 1)
    for b in range(2):

        def start1(d, carry):
            peer = lax.rem(g + d, GX)
            copy1(b, peer, g, peer).start()
            return carry

        lax.fori_loop(1, GX, start1, 0)
        recv1[b, g] = send1[b, g]

    loads[1].wait()
    waves = wave_ref[0:1, :]
    rows = lax.broadcasted_iota(jnp.int32, (48, 1024), 0)
    steps = jnp.where(rows < 32, rows * 64, jnp.where(rows < 40, rows - 32, (rows - 40) * 8))
    real, imag = cos_sin((steps * waves) & (N - 1))
    base_re[...] = real
    base_im[...] = imag

    def table(step, carry):
        group, c = step // 8, lax.rem(step, 8)
        cols = pl.ds(pl.multiple_of(128 * c, 128), 128)
        tile = pl.ds(pl.multiple_of(8 * group, 8), 8)
        tile_re, tile_im = base_re[tile, cols], base_im[tile, cols]
        br, bi = base_re[32:40, cols], base_im[32:40, cols]
        for i in range(0, 8, 2):
            both_re, both_im = [], []
            for k in (i, i + 1):
                ar, ai = tile_re[k : k + 1], tile_im[k : k + 1]
                both_re.append(ar * br - ai * bi)
                both_im.append(-(ar * bi + ai * br))
            re_hi, re_lo = split(jnp.concatenate(both_re, axis=0))
            im_hi, im_lo = split(jnp.concatenate(both_im, axis=0))
            at = pl.multiple_of(group * 64 + i * 8, 16)
            tabs[c, pl.ds(at, 16), 0:128] = re_hi
            tabs[c, pl.ds(at, 16), 128:256] = im_hi
            tabs[c, pl.ds(at + 256, 16), 0:128] = re_lo
            tabs[c, pl.ds(at + 256, 16), 128:256] = im_lo
        return carry

    lax.fori_loop(0, 32, table, 0)

    def copy2(hf, b, owner, slot, zz):
        return pltpu.make_async_remote_copy(
            src_ref=send2.at[hf, b, owner], dst_ref=recv2.at[hf, b, slot],
            send_sem=s2.at[hf, b, owner], recv_sem=r2.at[hf, b, slot],
            device_id=(owner, zz), device_id_type=MESH,
        )

    my_slot = 4 * z + lax.rem(g, 4)

    def start2(hf, b, owner):
        place = lax.rem(level + owner // 4, GY)
        mine = (owner == g) & (place == z)

        @pl.when(jnp.logical_not(mine))
        def _():
            copy2(hf, b, owner, my_slot, place).start()

        @pl.when(mine)
        def _():
            recv2[hf, b, my_slot] = send2[hf, b, owner]

    for b in range(2):

        def wait1(d, carry):
            peer = lax.rem(g + d, GX)
            copy1(b, peer, peer, peer).wait_recv()
            return carry

        lax.fori_loop(1, GX, wait1, 0)
        for i in range(2):
            hi, lo = split(recv1[b, 16 * i : 16 * i + 16].reshape(128, 256).T)
            lhs[:, pl.ds(128 * i, 128)] = hi
            lhs[:, pl.ds(256 + 128 * i, 128)] = hi
            lhs[:, pl.ds(512 + 128 * i, 128)] = lo

        def chunk(step, carry):
            c = lax.rem(step + level, 8)
            sums = jnp.dot(lhs[:, 0:512], tabs[c], preferred_element_type=F32)
            sums = sums + jnp.dot(lhs[:, 512:768], tabs[c, 0:256, :], preferred_element_type=F32)
            cols = pl.ds(pl.multiple_of(128 * c, 128), 128)
            tre, tim = base_re[40:48, cols], base_im[40:48, cols]
            xr, xi = sums[0:32, 0:128], sums[0:32, 128:256]
            for h in range(1, 8):
                gr, gi = sums[32 * h : 32 * h + 32, 0:128], sums[32 * h : 32 * h + 32, 128:256]
                cr, ci = tre[h : h + 1], tim[h : h + 1]
                xr = xr + gr * cr + gi * ci
                xi = xi + gi * cr - gr * ci
            parts = [x[8 * v : 8 * v + 8] for v in range(4) for x in (xr, xi)]
            for i, block in enumerate(swap_blocks(parts, lane)):
                send2[i % 2, b, 4 * c + i // 2] = block
            for d in range(4):
                start2(0, b, 4 * c + d)
            return carry

        lax.fori_loop(0, 8, chunk, 0)

        def rest(i, carry):
            start2(1, b, lax.rem(4 * level + i, GX))
            return carry

        lax.fori_loop(0, GX, rest, 0)

        def drain1(d, carry):
            peer = lax.rem(g + d, GX)
            copy1(b, peer, peer, peer).wait_send()
            return carry

        lax.fori_loop(1, GX, drain1, 0)

    for i in (3, 4, 2):
        loads[i].wait()
    weight = mask_ref[...].astype(F32)

    def copy3(hf, src, slot, peer):
        return pltpu.make_async_remote_copy(
            src_ref=send3.at[hf, src], dst_ref=recv3.at[hf, slot], send_sem=s3.at[hf, src], recv_sem=r3.at[hf, slot],
            device_id=(g, peer), device_id_type=MESH,
        )

    for hf in range(2):
        for b in range(2):

            def wait2(slot, carry):
                source = 4 * my_level + lax.rem(slot, 4)
                mine = (source == g) & (slot // 4 == z)

                @pl.when(jnp.logical_not(mine))
                def _():
                    copy2(hf, b, 0, slot, z).wait_recv()

                return carry

            lax.fori_loop(0, 32, wait2, 0)
            hi, lo = split(recv2[hf, b].reshape(256, 128).T)
            both = jnp.concatenate([hi, hi, lo], axis=1)
            ybuf[pl.ds(128 * b, 128), :] = jnp.dot(both, w_ref[...], preferred_element_type=F32)

        def finish(tile, carry):
            at = pl.multiple_of(8 * tile, 8)
            values = []
            for v in range(8):
                rr = ybuf[pl.ds(32 * v + at, 8), :]
                ii = ybuf[pl.ds(32 * v + 16 + at, 8), :]
                re = rr[:, :256] - ii[:, 256:]
                im = rr[:, 256:] + ii[:, :256]
                c, s = twiddle_ref[v : v + 1, :], twiddle_ref[8 + v : 9 + v, :]
                values.append((re * c + im * s, im * c - re * s))
            for q, (re, im) in enumerate(eight_points(values)):
                send3[hf, q, 0, pl.ds(at, 8), :] = re
                send3[hf, q, 1, pl.ds(at, 8), :] = im
            return carry

        lax.fori_loop(0, 2, finish, 0)
        for d in range(1, GY):
            peer = lax.rem(z + d, GY)
            copy3(hf, peer, z, peer).start()

    for hf in range(2):
        rows = pl.ds(16 * hf, 16)
        for p in range(2):
            out_ref[p, my_level, rows] = send3[hf, z, p] * weight[16 * hf : 16 * hf + 16]
        for b in range(2):

            def drain2(owner, carry):
                place = lax.rem(level + owner // 4, GY)
                mine = (owner == g) & (place == z)

                @pl.when(jnp.logical_not(mine))
                def _():
                    copy2(hf, b, owner, my_slot, place).wait_send()

                return carry

            lax.fori_loop(0, GX, drain2, 0)
    for hf in range(2):
        rows = pl.ds(16 * hf, 16)
        for d in range(1, GY):
            peer = lax.rem(z + d, GY)
            copy3(hf, peer, peer, peer).wait_recv()
            for p in range(2):
                out_ref[p, lax.rem(my_level + d, GY), rows] = recv3[hf, peer, p] * weight[16 * hf : 16 * hf + 16]
    for hf in range(2):
        for d in range(1, GY):
            peer = lax.rem(z + d, GY)
            copy3(hf, peer, peer, peer).wait_send()


def y_tables():
    turns = np.outer(np.arange(256), np.arange(256)) % 256 * (2.0 * np.pi / 256)
    table = np.concatenate([np.cos(turns), -np.sin(turns)], axis=1).astype(np.float32)
    high = table.astype(jnp.bfloat16)
    low = (table - high.astype(np.float32)).astype(jnp.bfloat16)
    angles = np.outer(np.arange(8), np.arange(256)) * (2.0 * np.pi / N)
    twiddle = np.concatenate([np.cos(angles), np.sin(angles)]) / N
    return np.concatenate([high, low, high], axis=0), twiddle.astype(np.float32)


def shards(fields, wave_order, kept_mask):
    w, twiddle = y_tables()
    vmem = pl.BlockSpec(memory_space=pltpu.VMEM)
    dma = pltpu.SemaphoreType.DMA
    return pl.pallas_call(
        kernel,
        out_shape=jax.ShapeDtypeStruct((2, 8, 32, 256), F32),
        in_specs=[pl.BlockSpec(memory_space=pltpu.HBM)] * 5,
        out_specs=vmem,
        scratch_shapes=[
            pltpu.VMEM((8, 64, 256), F32),
            pltpu.VMEM((1, 1024), jnp.int32),
            pltpu.VMEM((32, 256), jnp.int32),
            pltpu.VMEM((768, 512), BF16),
            pltpu.VMEM((16, 256), F32),
            dma((5,)),
            pltpu.VMEM((2, 32, 8, 256), F32),
            pltpu.VMEM((2, 32, 8, 256), F32),
            pltpu.VMEM((48, 1024), F32),
            pltpu.VMEM((48, 1024), F32),
            pltpu.VMEM((8, 512, 256), BF16),
            pltpu.VMEM((256, 768), BF16),
            pltpu.VMEM((2, 2, 32, 8, 128), F32),
            pltpu.VMEM((2, 2, 32, 8, 128), F32),
            pltpu.VMEM((256, 512), F32),
            pltpu.VMEM((2, 8, 2, 16, 256), F32),
            pltpu.VMEM((2, 8, 2, 16, 256), F32),
            dma((2, 32)), dma((2, 32)), dma((2, 2, 32)), dma((2, 2, 32)), dma((2, 8)), dma((2, 8)),
        ],
        compiler_params=pltpu.CompilerParams(has_side_effects=True, collective_id=0, vmem_limit_bytes=67043328),
        name="bifourier",
    )(fields, wave_order.reshape(1, 1024), kept_mask, jnp.asarray(w), jnp.asarray(twiddle))


def solution(mesh):
    return jax.shard_map(
        shards,
        mesh=mesh,
        in_specs=(P(None, "gx", "gy"), P(), P("gx", "gy")),
        out_specs=P(None, None, "gx", "gy"),
        check_vma=False,
    )
```

time: 55.6 us -> 54.5 us (0.980)
  Pallas kernels: 53.1 us -> 52.5 us
    pallas_call x1, Pallas kernels: 53.1 us -> 52.5 us  [shards(): pl.pallas_call(kernel, out_shape=jax.ShapeDtypeStruct((2, 8, 32, 256), F3...]
where the time goes in v4:
time: 54.5 us; the launch traced here: 54.3 us
  Pallas kernels  52.5 us (96%)
  local copies, waits for them, and re-layouts  1.88 us (3%)
    pallas_call x1, Pallas kernels, shards(): pl.pallas_call(kernel, out_shape=jax.ShapeDtypeStruct((2, 8, 32, 256), F3...  52.5 us
    unnamed x1, local copies, waits for them, and re-layouts  1.88 us

profile of v4, /device:TPU:1, one launch (start us, length us, event | category | flops | bytes accessed | tf_op | source)
XLA Modules:
  0.0 54.3 jit_solution(13614036338281284161)
XLA Ops:
  0.0 52.5 %bifourier.1 = f32[2,8,32,256]{3,2,1,0:T(8,128)} custom-call(f32[8,64,256]{2,1,0:T(8,128)} %fields_hbm.1, s32[1,1024]{1,0:T(1,128)} %bitcast.1, s32[32,256]{1,0:T(8,128)} %mask_hbm.1, bf16[768,512]{1,0:T(8,128)(2,1)} %constant.4.clone.w_hbm, f32[16,256]{1,0:T(8,128)} %constant.5.clone.twiddle_hbm), custom_call_target="tpu_custom_call" | custom-call | tf_op jit(solution)/shard_map/bifourier/pallas_call | solution.py:339
  52.5 1.9 %copy.7 = f32[2,8,32,256]{3,2,1,0:T(8,128)} copy(f32[2,8,32,256]{3,2,1,0:T(8,128)} %bifourier.1) | data formatting | bytes 1048576

commit v5 on v4

--- a/solution.py
+++ b/solution.py
@@ -1,4 +1,3 @@
-import functools
 import math
 
 import jax
@@ -81,21 +80,33 @@
     return values
 
 
+def place_of(level, owner):
+    sign = 1 - 2 * lax.rem(owner, 2)
+    high = lax.rem(lax.rem(owner // 2, 4) + sign * (level // 2 - owner // 8) + 8, 4)
+    return 2 * high + lax.rem(level + owner, 2)
+
+
+def level_of(owner, place):
+    sign = 1 - 2 * lax.rem(owner, 2)
+    high = lax.rem(owner // 8 + sign * (place // 2 - lax.rem(owner // 2, 4)) + 8, 4)
+    return 2 * high + lax.rem(place + owner, 2)
+
+
 def kernel(
-    fields_hbm, wave_hbm, mask_hbm, w_hbm, twiddle_hbm, out_ref,
-    fields_ref, wave_ref, mask_ref, w_ref, twiddle_ref, load,
+    fields_hbm, wave_hbm, w_hbm, twiddle_hbm, mask_hbm, out_ref, weight_hbm,
+    fields_ref, wave_ref, w_ref, twiddle_ref, mask_ref, weight_ref, load,
     send1, recv1, base_re, base_im, tabs, lhs, send2, recv2, ybuf, send3, recv3,
-    s1, r1, s2, r2, s3, r3,
+    s1, r1, s2, r2, s3, r3, own_sem,
 ):
     g = lax.axis_index("gx")
     z = lax.axis_index("gy")
     level = g // 4
-    my_level = lax.rem(z + GY - level, GY)
+    my_level = level_of(g, z)
 
     loads = [
         pltpu.make_async_copy(source, target, load.at[i])
         for i, (source, target) in enumerate(
-            [(fields_hbm, fields_ref), (wave_hbm, wave_ref), (mask_hbm, mask_ref), (w_hbm, w_ref), (twiddle_hbm, twiddle_ref)]
+            [(fields_hbm, fields_ref), (wave_hbm, wave_ref), (w_hbm, w_ref), (twiddle_hbm, twiddle_ref), (mask_hbm, mask_ref)]
         )
     ]
     for copy in loads:
@@ -129,13 +140,11 @@
 
     def copy1(b, src, slot, peer):
         return pltpu.make_async_remote_copy(
-            src_ref=send1.at[b, src], dst_ref=recv1.at[b, slot], send_sem=s1.at[b, src], recv_sem=r1.at[b, slot],
+            src_ref=send1.at[b, src], dst_ref=recv1.at[b, slot], send_sem=s1.at[b], recv_sem=r1.at[b],
             device_id=(peer, z), device_id_type=MESH,
         )
 
-    pl.semaphore_wait(barrier, GX - 1 + GY - 1)
-    for b in range(2):
-
+    def send_all(b):
         def start1(d, carry):
             peer = lax.rem(g + d, GX)
             copy1(b, peer, g, peer).start()
@@ -143,6 +152,9 @@
 
         lax.fori_loop(1, GX, start1, 0)
         recv1[b, g] = send1[b, g]
+
+    pl.semaphore_wait(barrier, GX - 1 + GY - 1)
+    send_all(0)
 
     loads[1].wait()
     waves = wave_ref[0:1, :]
@@ -174,36 +186,60 @@
         return carry
 
     lax.fori_loop(0, 32, table, 0)
-
-    def copy2(hf, b, owner, slot, zz):
+    send_all(1)
+
+    def copy2(part, owner, slot, zz):
+        at = (lambda ref, i: ref.at[0, i, part]) if part < 2 else (lambda ref, i: ref.at[1, i])
         return pltpu.make_async_remote_copy(
-            src_ref=send2.at[hf, b, owner], dst_ref=recv2.at[hf, b, slot],
-            send_sem=s2.at[hf, b, owner], recv_sem=r2.at[hf, b, slot],
+            src_ref=at(send2, owner), dst_ref=at(recv2, slot), send_sem=s2.at[part], recv_sem=r2.at[part],
             device_id=(owner, zz), device_id_type=MESH,
         )
 
     my_slot = 4 * z + lax.rem(g, 4)
 
-    def start2(hf, b, owner):
-        place = lax.rem(level + owner // 4, GY)
-        mine = (owner == g) & (place == z)
-
-        @pl.when(jnp.logical_not(mine))
+    stays = my_level == level
+
+    def start2(part, owner):
+        copy2(part, owner, my_slot, place_of(level, owner)).start()
+
+    def start2_own(part):
+        @pl.when(jnp.logical_not(stays))
         def _():
-            copy2(hf, b, owner, my_slot, place).start()
-
-        @pl.when(mine)
+            start2(part, g)
+
+        @pl.when(stays)
         def _():
-            recv2[hf, b, my_slot] = send2[hf, b, owner]
+            if part < 2:
+                recv2[0, my_slot, part] = send2[0, g, part]
+            else:
+                recv2[1, my_slot] = send2[1, g]
+
+    def each_size(wait):
+        @pl.when(stays)
+        def _():
+            wait(GX - 1)
+
+        @pl.when(jnp.logical_not(stays))
+        def _():
+            wait(GX)
+
+    def group(source, target, send_sem, recv_sem):
+        return pltpu.make_async_remote_copy(
+            src_ref=source, dst_ref=target, send_sem=send_sem, recv_sem=recv_sem, device_id=(g, z), device_id_type=MESH
+        )
+
+    def all1(b):
+        part = pl.ds(0, GX - 1)
+        return group(send1.at[b, part], recv1.at[b, part], s1.at[b], r1.at[b])
+
+    def all2(part, count):
+        first = pl.ds(0, count)
+        at = (lambda ref: ref.at[0, first, part]) if part < 2 else (lambda ref: ref.at[1, first])
+        return group(at(send2), at(recv2), s2.at[part], r2.at[part])
 
     for b in range(2):
 
-        def wait1(d, carry):
-            peer = lax.rem(g + d, GX)
-            copy1(b, peer, peer, peer).wait_recv()
-            return carry
-
-        lax.fori_loop(1, GX, wait1, 0)
+        all1(b).wait_recv()
         for i in range(2):
             hi, lo = split(recv1[b, 16 * i : 16 * i + 16].reshape(128, 256).T)
             lhs[:, pl.ds(128 * i, 128)] = hi
@@ -211,64 +247,68 @@
             lhs[:, pl.ds(512 + 128 * i, 128)] = lo
 
         def chunk(step, carry):
-            c = lax.rem(step + level, 8)
-            sums = jnp.dot(lhs[:, 0:512], tabs[c], preferred_element_type=F32)
-            sums = sums + jnp.dot(lhs[:, 512:768], tabs[c, 0:256, :], preferred_element_type=F32)
-            cols = pl.ds(pl.multiple_of(128 * c, 128), 128)
-            tre, tim = base_re[40:48, cols], base_im[40:48, cols]
-            xr, xi = sums[0:32, 0:128], sums[0:32, 128:256]
-            for h in range(1, 8):
-                gr, gi = sums[32 * h : 32 * h + 32, 0:128], sums[32 * h : 32 * h + 32, 128:256]
-                cr, ci = tre[h : h + 1], tim[h : h + 1]
-                xr = xr + gr * cr + gi * ci
-                xi = xi + gi * cr - gr * ci
-            parts = [x[8 * v : 8 * v + 8] for v in range(4) for x in (xr, xi)]
-            for i, block in enumerate(swap_blocks(parts, lane)):
-                send2[i % 2, b, 4 * c + i // 2] = block
-            for d in range(4):
-                start2(0, b, 4 * c + d)
+            for k in range(2):
+                c = lax.rem(2 * step + k + level, 8)
+                sums = jnp.dot(lhs[:, 0:512], tabs[c], preferred_element_type=F32)
+                sums = sums + jnp.dot(lhs[:, 512:768], tabs[c, 0:256, :], preferred_element_type=F32)
+                cols = pl.ds(pl.multiple_of(128 * c, 128), 128)
+                tre, tim = base_re[40:48, cols], base_im[40:48, cols]
+                xr, xi = sums[0:32, 0:128], sums[0:32, 128:256]
+                for h in range(1, 8):
+                    gr, gi = sums[32 * h : 32 * h + 32, 0:128], sums[32 * h : 32 * h + 32, 128:256]
+                    cr, ci = tre[h : h + 1], tim[h : h + 1]
+                    xr = xr + gr * cr + gi * ci
+                    xi = xi + gi * cr - gr * ci
+                parts = [x[8 * v : 8 * v + 8] for v in range(4) for x in (xr, xi)]
+                for i, block in enumerate(swap_blocks(parts, lane)):
+                    send2[i % 2, 4 * c + i // 2, b] = block
+            for k in range(2):
+                c = lax.rem(2 * step + k + level, 8)
+                for d in range(4):
+                    owner = 4 * c + lax.rem(g + d, 4)
+                    if k == 0 and d == 0:
+
+                        @pl.when(step > 0)
+                        def _():
+                            start2(b, owner)
+
+                    else:
+                        start2(b, owner)
+
+            @pl.when(step == 0)
+            def _():
+                start2_own(b)
+
             return carry
 
-        lax.fori_loop(0, 8, chunk, 0)
-
-        def rest(i, carry):
-            start2(1, b, lax.rem(4 * level + i, GX))
-            return carry
-
-        lax.fori_loop(0, GX, rest, 0)
-
-        def drain1(d, carry):
-            peer = lax.rem(g + d, GX)
-            copy1(b, peer, peer, peer).wait_send()
-            return carry
-
-        lax.fori_loop(1, GX, drain1, 0)
-
-    for i in (3, 4, 2):
+        lax.fori_loop(0, 4, chunk, 0)
+
+    def rest(d, carry):
+        start2(2, lax.rem(g + d, GX))
+        return carry
+
+    lax.fori_loop(1, GX, rest, 0)
+    start2_own(2)
+
+    for i in (2, 3, 4):
         loads[i].wait()
-    weight = mask_ref[...].astype(F32)
-
-    def copy3(hf, src, slot, peer):
+    weight_ref[...] = mask_ref[...].astype(F32)
+
+    def copy3(hf, src, peer):
         return pltpu.make_async_remote_copy(
-            src_ref=send3.at[hf, src], dst_ref=recv3.at[hf, slot], send_sem=s3.at[hf, src], recv_sem=r3.at[hf, slot],
-            device_id=(g, peer), device_id_type=MESH,
+            src_ref=send3.at[hf, src], dst_ref=out_ref.at[:, my_level, pl.ds(16 * hf, 16)],
+            send_sem=s3.at[hf], recv_sem=r3.at[hf], device_id=(g, peer), device_id_type=MESH,
         )
+
+    def own(hf):
+        return pltpu.make_async_copy(send3.at[hf, z], out_ref.at[:, my_level, pl.ds(16 * hf, 16)], own_sem.at[hf])
 
     for hf in range(2):
         for b in range(2):
 
-            def wait2(slot, carry):
-                source = 4 * my_level + lax.rem(slot, 4)
-                mine = (source == g) & (slot // 4 == z)
-
-                @pl.when(jnp.logical_not(mine))
-                def _():
-                    copy2(hf, b, 0, slot, z).wait_recv()
-
-                return carry
-
-            lax.fori_loop(0, 32, wait2, 0)
-            hi, lo = split(recv2[hf, b].reshape(256, 128).T)
+            if hf == 0 or b == 0:
+                each_size(lambda count: all2(2 * hf + b, count).wait_recv())
+            hi, lo = split(recv2[hf, :, b].reshape(256, 128).T)
             both = jnp.concatenate([hi, hi, lo], axis=1)
             ybuf[pl.ds(128 * b, 128), :] = jnp.dot(both, w_ref[...], preferred_element_type=F32)
 
@@ -288,38 +328,24 @@
             return carry
 
         lax.fori_loop(0, 2, finish, 0)
+        own(hf).start()
         for d in range(1, GY):
             peer = lax.rem(z + d, GY)
-            copy3(hf, peer, z, peer).start()
-
+            copy3(hf, peer, peer).start()
+
+    weight_out = pltpu.make_async_copy(weight_ref, weight_hbm, load.at[0])
+    weight_out.start()
+    for b in range(2):
+        all1(b).wait_send()
+    for part in range(3):
+        each_size(lambda count: all2(part, count).wait_send())
     for hf in range(2):
-        rows = pl.ds(16 * hf, 16)
-        for p in range(2):
-            out_ref[p, my_level, rows] = send3[hf, z, p] * weight[16 * hf : 16 * hf + 16]
-        for b in range(2):
-
-            def drain2(owner, carry):
-                place = lax.rem(level + owner // 4, GY)
-                mine = (owner == g) & (place == z)
-
-                @pl.when(jnp.logical_not(mine))
-                def _():
-                    copy2(hf, b, owner, my_slot, place).wait_send()
-
-                return carry
-
-            lax.fori_loop(0, GX, drain2, 0)
-    for hf in range(2):
-        rows = pl.ds(16 * hf, 16)
-        for d in range(1, GY):
-            peer = lax.rem(z + d, GY)
-            copy3(hf, peer, peer, peer).wait_recv()
-            for p in range(2):
-                out_ref[p, lax.rem(my_level + d, GY), rows] = recv3[hf, peer, p] * weight[16 * hf : 16 * hf + 16]
-    for hf in range(2):
-        for d in range(1, GY):
-            peer = lax.rem(z + d, GY)
-            copy3(hf, peer, peer, peer).wait_send()
+        own(hf).wait()
+        arrived = out_ref.at[:, pl.ds(0, GY - 1), pl.ds(16 * hf, 16)]
+        both = group(send3.at[hf, pl.ds(0, GY - 1)], arrived, s3.at[hf], r3.at[hf])
+        both.wait_recv()
+        both.wait_send()
+    weight_out.wait()
 
 
 def y_tables():
@@ -334,19 +360,19 @@
 
 def shards(fields, wave_order, kept_mask):
     w, twiddle = y_tables()
-    vmem = pl.BlockSpec(memory_space=pltpu.VMEM)
     dma = pltpu.SemaphoreType.DMA
-    return pl.pallas_call(
+    result, weight = pl.pallas_call(
         kernel,
-        out_shape=jax.ShapeDtypeStruct((2, 8, 32, 256), F32),
+        out_shape=[jax.ShapeDtypeStruct((2, 8, 32, 256), F32), jax.ShapeDtypeStruct((32, 256), F32)],
         in_specs=[pl.BlockSpec(memory_space=pltpu.HBM)] * 5,
-        out_specs=vmem,
+        out_specs=[pl.BlockSpec(memory_space=pltpu.HBM)] * 2,
         scratch_shapes=[
             pltpu.VMEM((8, 64, 256), F32),
             pltpu.VMEM((1, 1024), jnp.int32),
-            pltpu.VMEM((32, 256), jnp.int32),
             pltpu.VMEM((768, 512), BF16),
             pltpu.VMEM((16, 256), F32),
+            pltpu.VMEM((32, 256), jnp.int32),
+            pltpu.VMEM((32, 256), F32),
             dma((5,)),
             pltpu.VMEM((2, 32, 8, 256), F32),
             pltpu.VMEM((2, 32, 8, 256), F32),
@@ -354,16 +380,17 @@
             pltpu.VMEM((48, 1024), F32),
             pltpu.VMEM((8, 512, 256), BF16),
             pltpu.VMEM((256, 768), BF16),
-            pltpu.VMEM((2, 2, 32, 8, 128), F32),
-            pltpu.VMEM((2, 2, 32, 8, 128), F32),
+            pltpu.VMEM((2, 32, 2, 8, 128), F32),
+            pltpu.VMEM((2, 32, 2, 8, 128), F32),
             pltpu.VMEM((256, 512), F32),
             pltpu.VMEM((2, 8, 2, 16, 256), F32),
             pltpu.VMEM((2, 8, 2, 16, 256), F32),
-            dma((2, 32)), dma((2, 32)), dma((2, 2, 32)), dma((2, 2, 32)), dma((2, 8)), dma((2, 8)),
+            dma((2,)), dma((2,)), dma((3,)), dma((3,)), dma((2,)), dma((2,)), dma((2,)),
         ],
         compiler_params=pltpu.CompilerParams(has_side_effects=True, collective_id=0, vmem_limit_bytes=67043328),
         name="bifourier",
-    )(fields, wave_order.reshape(1, 1024), kept_mask, jnp.asarray(w), jnp.asarray(twiddle))
+    )(fields, wave_order.reshape(1, 1024), jnp.asarray(w), jnp.asarray(twiddle), kept_mask)
+    return result * weight
 
 
 def solution(mesh):

time: 54.5 us -> 47.4 us (0.87)
  Pallas kernels: 52.5 us -> 45.4 us
  other arithmetic: 0 us -> 1.88 us
  local copies, waits for them, and re-layouts: 1.88 us -> 0 us
    pallas_call x1, Pallas kernels: 52.5 us -> 45.4 us  [shards(): pl.pallas_call(kernel, out_shape=[jax.ShapeDtypeStruct((2, 8, 32, 256), F...]
    mul x0 -> x1, other arithmetic: none -> 1.88 us  [shards(): return result * weight]
    unnamed x1 -> x0, local copies, waits for them, and re-layouts: 1.88 us -> none
where the time goes in v5:
time: 47.4 us; the launch traced here: 47.2 us
  Pallas kernels  45.4 us (96%)
  other arithmetic  1.88 us (4%)
    pallas_call x1, Pallas kernels, shards(): pl.pallas_call(kernel, out_shape=[jax.ShapeDtypeStruct((2, 8, 32, 256), F...  45.4 us
    mul x1, other arithmetic, shards(): return result * weight  1.88 us

profile of v5, /device:TPU:1, one launch (start us, length us, event | category | flops | bytes accessed | tf_op | source)
XLA Modules:
  0.0 47.2 jit_solution(15744292161211871596)
XLA Ops:
  0.0 45.4 %bifourier.1 = (f32[2,8,32,256]{3,2,1,0:T(8,128)}, f32[32,256]{1,0:T(8,128)}) custom-call(f32[8,64,256]{2,1,0:T(8,128)} %fields_hbm.1, s32[1,1024]{1,0:T(1,128)} %bitcast.1, bf16[768,512]{1,0:T(8,128)(2,1)} %constant.4.clone.w_hbm, f32[16,256]{1,0:T(8,128)} %constant.5.clone.twiddle_hbm, s32[32,256]{1,0:T(8,128)} %mask_hbm.1), custom_call_target="tpu_custom_call" | custom-call | tf_op jit(solution)/shard_map/bifourier/pallas_call | solution.py:364
  45.4 1.9 %broadcast_multiply_fusion = f32[2,8,32,256]{3,2,1,0:T(8,128)} fusion(f32[2,8,32,256]{3,2,1,0:T(8,128)} %get-tuple-element.7, f32[32,256]{1,0:T(8,128)} %get-tuple-element.8), kind=kLoop, calls=%fused_computation | loop fusion | flops 131072 | bytes 1081344 | tf_op jit(solution)/shard_map/mul | solution.py:393

commit v6 on v5

--- a/solution.py
+++ b/solution.py
@@ -14,6 +14,7 @@
 N = 2048
 GX = 32
 GY = 8
+FAR_FIRST = (4, 3, 5, 2, 6, 1, 7)
 
 
 def split(value):
@@ -92,6 +93,24 @@
     return 2 * high + lax.rem(place + owner, 2)
 
 
+def far_first(j):
+    return lax.rem(10 - j + 3 * (j * (j - 1) // 2), 4)
+
+
+def each_peer(g, visit):
+    inner = [2 * lax.rem(g // 2 + shift, 4) + lax.rem(g + 1 + k, 2) for shift in (2, 1, 3, 0) for k in range(2)]
+
+    def column(j, carry):
+        first = 8 * lax.rem(g // 8 + far_first(j), 4)
+        for offset in inner:
+            visit(first + offset)
+        return carry
+
+    lax.fori_loop(0, 3, column, 0)
+    for offset in inner[:-1]:
+        visit(8 * (g // 8) + offset)
+
+
 def kernel(
     fields_hbm, wave_hbm, w_hbm, twiddle_hbm, mask_hbm, out_ref, weight_hbm,
     fields_ref, wave_ref, w_ref, twiddle_ref, mask_ref, weight_ref, load,
@@ -114,29 +133,31 @@
 
     barrier = pltpu.get_barrier_semaphore()
 
-    def greet(d, carry):
-        pl.semaphore_signal(barrier, inc=1, device_id=(lax.rem(g + d, GX), z), device_id_type=MESH)
-        return carry
-
-    lax.fori_loop(1, GX, greet, 0)
-    for d in range(1, GY):
+    def greet(peer):
+        pl.semaphore_signal(barrier, inc=1, device_id=(peer, z), device_id_type=MESH)
+
+    each_peer(g, greet)
+    for d in FAR_FIRST:
         pl.semaphore_signal(barrier, inc=1, device_id=(g, lax.rem(z + d, GY)), device_id_type=MESH)
     lane = lax.broadcasted_iota(jnp.int32, (8, 128), 1)
     order = (lane & 64) + ((lane & 7) << 3) + ((lane >> 3) & 7)
     loads[0].wait()
 
-    def pack(s, carry):
-        for j in range(2):
-            for quad in range(2):
-                part = [
-                    jnp.take_along_axis(fields_ref[s, pl.ds(32 * quad + 8 * h, 8), pl.ds(128 * j, 128)], order, axis=1)
-                    for h in range(4)
-                ]
-                for d, block in enumerate(swap_blocks(part, lane)):
-                    send1[d % 2, 4 * s + 2 * j + d // 2, :, pl.ds(128 * quad, 128)] = block
+    def pack(step, carry):
+        for s in (2 * step, 2 * step + 1):
+            for j in range(2):
+                for quad in range(2):
+                    part = [
+                        jnp.take_along_axis(
+                            fields_ref[s, pl.ds(32 * quad + 8 * h, 8), pl.ds(128 * j, 128)], order, axis=1
+                        )
+                        for h in range(4)
+                    ]
+                    for d, block in enumerate(swap_blocks(part, lane)):
+                        send1[d % 2, 4 * s + 2 * j + d // 2, :, pl.ds(128 * quad, 128)] = block
         return carry
 
-    lax.fori_loop(0, 8, pack, 0)
+    lax.fori_loop(0, 4, pack, 0)
 
     def copy1(b, src, slot, peer):
         return pltpu.make_async_remote_copy(
@@ -145,12 +166,7 @@
         )
 
     def send_all(b):
-        def start1(d, carry):
-            peer = lax.rem(g + d, GX)
-            copy1(b, peer, g, peer).start()
-            return carry
-
-        lax.fori_loop(1, GX, start1, 0)
+        each_peer(g, lambda peer: copy1(b, peer, g, peer).start())
         recv1[b, g] = send1[b, g]
 
     pl.semaphore_wait(barrier, GX - 1 + GY - 1)
@@ -248,7 +264,7 @@
 
         def chunk(step, carry):
             for k in range(2):
-                c = lax.rem(2 * step + k + level, 8)
+                c = 2 * lax.rem(g // 8 + far_first(step), 4) + lax.rem(level + 1 + k, 2)
                 sums = jnp.dot(lhs[:, 0:512], tabs[c], preferred_element_type=F32)
                 sums = sums + jnp.dot(lhs[:, 512:768], tabs[c, 0:256, :], preferred_element_type=F32)
                 cols = pl.ds(pl.multiple_of(128 * c, 128), 128)
@@ -263,19 +279,19 @@
                 for i, block in enumerate(swap_blocks(parts, lane)):
                     send2[i % 2, 4 * c + i // 2, b] = block
             for k in range(2):
-                c = lax.rem(2 * step + k + level, 8)
+                c = 2 * lax.rem(g // 8 + far_first(step), 4) + lax.rem(level + 1 + k, 2)
                 for d in range(4):
                     owner = 4 * c + lax.rem(g + d, 4)
-                    if k == 0 and d == 0:
-
-                        @pl.when(step > 0)
+                    if k == 1 and d == 0:
+
+                        @pl.when(step < 3)
                         def _():
                             start2(b, owner)
 
                     else:
                         start2(b, owner)
 
-            @pl.when(step == 0)
+            @pl.when(step == 3)
             def _():
                 start2_own(b)
 
@@ -283,11 +299,7 @@
 
         lax.fori_loop(0, 4, chunk, 0)
 
-    def rest(d, carry):
-        start2(2, lax.rem(g + d, GX))
-        return carry
-
-    lax.fori_loop(1, GX, rest, 0)
+    each_peer(g, lambda owner: start2(2, owner))
     start2_own(2)
 
     for i in (2, 3, 4):
@@ -329,7 +341,7 @@
 
         lax.fori_loop(0, 2, finish, 0)
         own(hf).start()
-        for d in range(1, GY):
+        for d in FAR_FIRST:
             peer = lax.rem(z + d, GY)
             copy3(hf, peer, peer).start()
 

time: 47.4 us -> 45.4 us (0.958)
  Pallas kernels: 45.4 us -> 43.4 us
    pallas_call x1, Pallas kernels: 45.4 us -> 43.4 us  [shards(): pl.pallas_call(kernel, out_shape=[jax.ShapeDtypeStruct((2, 8, 32, 256), F...]
where the time goes in v6:
time: 45.4 us; the launch traced here: 45.3 us
  Pallas kernels  43.4 us (96%)
  other arithmetic  1.88 us (4%)
    pallas_call x1, Pallas kernels, shards(): pl.pallas_call(kernel, out_shape=[jax.ShapeDtypeStruct((2, 8, 32, 256), F...  43.4 us
    mul x1, other arithmetic, shards(): return result * weight  1.88 us

profile of v6, /device:TPU:1, one launch (start us, length us, event | category | flops | bytes accessed | tf_op | source)
XLA Modules:
  0.0 45.3 jit_solution(7948601194548351755)
XLA Ops:
  0.0 43.4 %bifourier.1 = (f32[2,8,32,256]{3,2,1,0:T(8,128)}, f32[32,256]{1,0:T(8,128)}) custom-call(f32[8,64,256]{2,1,0:T(8,128)} %fields_hbm.1, s32[1,1024]{1,0:T(1,128)} %bitcast.1, bf16[768,512]{1,0:T(8,128)(2,1)} %constant.4.clone.w_hbm, f32[16,256]{1,0:T(8,128)} %constant.5.clone.twiddle_hbm, s32[32,256]{1,0:T(8,128)} %mask_hbm.1), custom_call_target="tpu_custom_call" | custom-call | tf_op jit(solution)/shard_map/bifourier/pallas_call | solution.py:376
  43.4 1.9 %broadcast_multiply_fusion = f32[2,8,32,256]{3,2,1,0:T(8,128)} fusion(f32[2,8,32,256]{3,2,1,0:T(8,128)} %get-tuple-element.7, f32[32,256]{1,0:T(8,128)} %get-tuple-element.8), kind=kLoop, calls=%fused_computation | loop fusion | flops 131072 | bytes 1081344 | tf_op jit(solution)/shard_map/mul | solution.py:405

commit v7 on v6

--- a/solution.py
+++ b/solution.py
@@ -112,8 +112,8 @@
 
 
 def kernel(
-    fields_hbm, wave_hbm, w_hbm, twiddle_hbm, mask_hbm, out_ref, weight_hbm,
-    fields_ref, wave_ref, w_ref, twiddle_ref, mask_ref, weight_ref, load,
+    fields_hbm, wave_hbm, w_hbm, out_ref,
+    fields_ref, wave_ref, w_ref, twiddle_ref, load,
     send1, recv1, base_re, base_im, tabs, lhs, send2, recv2, ybuf, send3, recv3,
     s1, r1, s2, r2, s3, r3, own_sem,
 ):
@@ -125,7 +125,7 @@
     loads = [
         pltpu.make_async_copy(source, target, load.at[i])
         for i, (source, target) in enumerate(
-            [(fields_hbm, fields_ref), (wave_hbm, wave_ref), (w_hbm, w_ref), (twiddle_hbm, twiddle_ref), (mask_hbm, mask_ref)]
+            [(fields_hbm, fields_ref), (wave_hbm, wave_ref), (w_hbm, w_ref)]
         )
     ]
     for copy in loads:
@@ -171,6 +171,11 @@
 
     pl.semaphore_wait(barrier, GX - 1 + GY - 1)
     send_all(0)
+
+    phase = lax.broadcasted_iota(jnp.int32, (8, 256), 0) * lax.broadcasted_iota(jnp.int32, (8, 256), 1)
+    real, imag = cos_sin(phase & (N - 1))
+    twiddle_ref[0:8, :] = real * (1.0 / N)
+    twiddle_ref[8:16, :] = imag * (1.0 / N)
 
     loads[1].wait()
     waves = wave_ref[0:1, :]
@@ -302,9 +307,7 @@
     each_peer(g, lambda owner: start2(2, owner))
     start2_own(2)
 
-    for i in (2, 3, 4):
-        loads[i].wait()
-    weight_ref[...] = mask_ref[...].astype(F32)
+    loads[2].wait()
 
     def copy3(hf, src, peer):
         return pltpu.make_async_remote_copy(
@@ -345,8 +348,6 @@
             peer = lax.rem(z + d, GY)
             copy3(hf, peer, peer).start()
 
-    weight_out = pltpu.make_async_copy(weight_ref, weight_hbm, load.at[0])
-    weight_out.start()
     for b in range(2):
         all1(b).wait_send()
     for part in range(3):
@@ -357,7 +358,6 @@
         both = group(send3.at[hf, pl.ds(0, GY - 1)], arrived, s3.at[hf], r3.at[hf])
         both.wait_recv()
         both.wait_send()
-    weight_out.wait()
 
 
 def y_tables():
@@ -365,27 +365,23 @@
     table = np.concatenate([np.cos(turns), -np.sin(turns)], axis=1).astype(np.float32)
     high = table.astype(jnp.bfloat16)
     low = (table - high.astype(np.float32)).astype(jnp.bfloat16)
-    angles = np.outer(np.arange(8), np.arange(256)) * (2.0 * np.pi / N)
-    twiddle = np.concatenate([np.cos(angles), np.sin(angles)]) / N
-    return np.concatenate([high, low, high], axis=0), twiddle.astype(np.float32)
+    return np.concatenate([high, low, high], axis=0)
 
 
 def shards(fields, wave_order, kept_mask):
-    w, twiddle = y_tables()
+    w = y_tables()
     dma = pltpu.SemaphoreType.DMA
-    result, weight = pl.pallas_call(
+    result = pl.pallas_call(
         kernel,
-        out_shape=[jax.ShapeDtypeStruct((2, 8, 32, 256), F32), jax.ShapeDtypeStruct((32, 256), F32)],
-        in_specs=[pl.BlockSpec(memory_space=pltpu.HBM)] * 5,
-        out_specs=[pl.BlockSpec(memory_space=pltpu.HBM)] * 2,
+        out_shape=jax.ShapeDtypeStruct((2, 8, 32, 256), F32),
+        in_specs=[pl.BlockSpec(memory_space=pltpu.HBM)] * 3,
+        out_specs=pl.BlockSpec(memory_space=pltpu.HBM),
         scratch_shapes=[
             pltpu.VMEM((8, 64, 256), F32),
             pltpu.VMEM((1, 1024), jnp.int32),
             pltpu.VMEM((768, 512), BF16),
             pltpu.VMEM((16, 256), F32),
-            pltpu.VMEM((32, 256), jnp.int32),
-            pltpu.VMEM((32, 256), F32),
-            dma((5,)),
+            dma((3,)),
             pltpu.VMEM((2, 32, 8, 256), F32),
             pltpu.VMEM((2, 32, 8, 256), F32),
             pltpu.VMEM((48, 1024), F32),
@@ -399,10 +395,11 @@
             pltpu.VMEM((2, 8, 2, 16, 256), F32),
             dma((2,)), dma((2,)), dma((3,)), dma((3,)), dma((2,)), dma((2,)), dma((2,)),
         ],
-        compiler_params=pltpu.CompilerParams(has_side_effects=True, collective_id=0, vmem_limit_bytes=67043328),
+        compiler_params=pltpu.CompilerParams(has_side_effects=True, collective_id=0, vmem_limit_bytes=int(67043328-10.75*1048576)),
         name="bifourier",
-    )(fields, wave_order.reshape(1, 1024), jnp.asarray(w), jnp.asarray(twiddle), kept_mask)
-    return result * weight
+    )(fields, wave_order.reshape(1, 1024), jnp.asarray(w))
+    bound = (result != result).astype(jnp.int32)
+    return jnp.where(kept_mask[None, None] > bound, result, 0.0)
 
 
 def solution(mesh):

time: 45.4 us -> 45 us (level)
  other arithmetic: 1.88 us -> 0.88 us
  local copies, waits for them, and re-layouts: 0 us -> 0.69 us
    mul x1 -> x0, other arithmetic: 1.88 us -> none  [shards(): return result * weight]
    select_n x0 -> x1, other arithmetic: none -> 0.88 us  [shards(): return jnp.where(kept_mask[None, None] > bound, result, 0.0)]
    unnamed x0 -> x4, local copies, waits for them, and re-layouts: none -> 0.69 us
where the time goes in v7:
time: 45 us; the launch traced here: 44.9 us
  Pallas kernels  43.3 us (96%)
  other arithmetic  0.88 us (2%)
  local copies, waits for them, and re-layouts  0.69 us (2%)
    pallas_call x1, Pallas kernels, shards(): pl.pallas_call(kernel, out_shape=jax.ShapeDtypeStruct((2, 8, 32, 256), F3...  43.3 us

profile of v7, /device:TPU:1, one launch (start us, length us, event | category | flops | bytes accessed | tf_op | source)
XLA Modules:
  0.0 44.9 jit_solution(9896827819295611908)
XLA Ops:
  0.0 0.0 copy-start
  0.0 0.7 %copy-done = s32[1024]{0:T(1024)S(1)} copy-done((s32[1024]{0:T(1024)S(1)}, s32[1024]{0:T(1024)}, u32[]{:S(2)}) %copy-start) | copy-done | bytes 4120
  0.7 0.0 copy-start.1
  0.7 43.3 %bifourier.1 = f32[2,8,32,256]{3,2,1,0:T(8,128)S(1)} custom-call(f32[8,64,256]{2,1,0:T(8,128)} %fields_hbm.1, s32[1,1024]{1,0:T(1,128)S(1)} %bitcast.1, bf16[768,512]{1,0:T(8,128)(2,1)} %constant.4.clone.w_hbm), custom_call_target="tpu_custom_call" | custom-call | tf_op jit(solution)/shard_map/bifourier/pallas_call | solution.py:374
  44.0 0.0 copy-done.1
  44.0 0.9 %fusion = f32[2,8,32,256]{3,2,1,0:T(8,128)} fusion(f32[2,8,32,256]{3,2,1,0:T(8,128)S(1)} %bifourier.1, s32[32,256]{1,0:T(8,128)S(1)} %copy-done.1), kind=kLoop, calls=%fused_computation.1 | loop fusion | flops 524288 | bytes 1081344 | tf_op jit(solution)/shard_map/jit(_where)/select_n | solution.py:402
Async XLA Ops:
  0.0 0.7 %copy-start = (s32[1024]{0:T(1024)S(1)}, s32[1024]{0:T(1024)}, u32[]{:S(2)}) copy-start(s32[1024]{0:T(1024)} %param.5) | copy-start | bytes 12292
  0.7 43.3 %copy-start.1 = (s32[32,256]{1,0:T(8,128)S(1)}, s32[32,256]{1,0:T(8,128)}, u32[]{:S(2)}) copy-start(s32[32,256]{1,0:T(8,128)} %param.6) | copy-start | bytes 98308

commit v8 on v7

--- a/solution.py
+++ b/solution.py
@@ -309,9 +309,9 @@
 
     loads[2].wait()
 
-    def copy3(hf, src, peer):
+    def copy3(hf, p, src, peer):
         return pltpu.make_async_remote_copy(
-            src_ref=send3.at[hf, src], dst_ref=out_ref.at[:, my_level, pl.ds(16 * hf, 16)],
+            src_ref=send3.at[hf, src, p], dst_ref=out_ref.at[p, my_level, pl.ds(16 * hf, 16)],
             send_sem=s3.at[hf], recv_sem=r3.at[hf], device_id=(g, peer), device_id_type=MESH,
         )
 
@@ -346,7 +346,8 @@
         own(hf).start()
         for d in FAR_FIRST:
             peer = lax.rem(z + d, GY)
-            copy3(hf, peer, peer).start()
+            for p in range(2):
+                copy3(hf, p, peer, peer).start()
 
     for b in range(2):
         all1(b).wait_send()

time: 45 us -> 45 us (level)
  no operation moved by 1% of the time
where the time goes in v8:
time: 45 us; the launch traced here: 44.9 us
  Pallas kernels  43.3 us (96%)
  other arithmetic  0.88 us (2%)
  local copies, waits for them, and re-layouts  0.69 us (2%)
    pallas_call x1, Pallas kernels, shards(): pl.pallas_call(kernel, out_shape=jax.ShapeDtypeStruct((2, 8, 32, 256), F3...  43.3 us

profile of v8, /device:TPU:1, one launch (start us, length us, event | category | flops | bytes accessed | tf_op | source)
XLA Modules:
  0.0 44.9 jit_solution(2149353505489623450)
XLA Ops:
  0.0 0.0 copy-start
  0.0 0.7 %copy-done = s32[1024]{0:T(1024)S(1)} copy-done((s32[1024]{0:T(1024)S(1)}, s32[1024]{0:T(1024)}, u32[]{:S(2)}) %copy-start) | copy-done | bytes 4120
  0.7 0.0 copy-start.1
  0.7 43.3 %bifourier.1 = f32[2,8,32,256]{3,2,1,0:T(8,128)S(1)} custom-call(f32[8,64,256]{2,1,0:T(8,128)} %fields_hbm.1, s32[1,1024]{1,0:T(1,128)S(1)} %bitcast.1, bf16[768,512]{1,0:T(8,128)(2,1)} %constant.4.clone.w_hbm), custom_call_target="tpu_custom_call" | custom-call | tf_op jit(solution)/shard_map/bifourier/pallas_call | solution.py:375
  44.0 0.0 copy-done.1
  44.0 0.9 %fusion = f32[2,8,32,256]{3,2,1,0:T(8,128)} fusion(f32[2,8,32,256]{3,2,1,0:T(8,128)S(1)} %bifourier.1, s32[32,256]{1,0:T(8,128)S(1)} %copy-done.1), kind=kLoop, calls=%fused_computation.1 | loop fusion | flops 524288 | bytes 1081344 | tf_op jit(solution)/shard_map/jit(_where)/select_n | solution.py:403
Async XLA Ops:
  0.0 0.7 %copy-start = (s32[1024]{0:T(1024)S(1)}, s32[1024]{0:T(1024)}, u32[]{:S(2)}) copy-start(s32[1024]{0:T(1024)} %param.5) | copy-start | bytes 12292
  0.7 43.3 %copy-start.1 = (s32[32,256]{1,0:T(8,128)S(1)}, s32[32,256]{1,0:T(8,128)}, u32[]{:S(2)}) copy-start(s32[32,256]{1,0:T(8,128)} %param.6) | copy-start | bytes 98308
